TPU v7x, 32 devices: a whole 2x2x4 slice. The times are simulated.
32 devices in a mesh: wide: 8 (over z, x), narrow: 4 (over y, core).
Axes of the slice: x: 2, y: 2, z: 4, core: 2. Of those that a mesh axis runs over, the one named last changes fastest.
Arguments:
- cost: float32 [1024, 16384], P('wide', 'narrow'), may hold values from 0 to 2
- plan: float32 [1024, 16384], P('wide', 'narrow'), may hold values from 0 to 2
- row_mass: float32 [1024], P('wide'), may hold values from 4096 to 28672
- col_mass: float32 [16384], P('narrow'), may hold values from 256 to 1792
- row_dual: float32 [1024], P('wide'), may hold values from -3 to 3
- col_dual: float32 [16384], P('narrow'), may hold values from -3 to 3
Outputs:
- plan_out: float32 [1024, 16384], P('wide', 'narrow')
- row_out: float32 [1024], P('wide')
- col_out: float32 [16384], P('narrow')
All inputs are finite; a program needn't handle non-finite values.
Results may differ from a plain program's by a relative error of at most 0.0001.
Values sent between devices are 32-bit elements; how exact they have to be, the bound alone decides.
A program may use at most 64 MiB of HBM per device.

v0:
```python
import math
import jax
import jax.numpy as jnp
from jax import lax
from jax.sharding import PartitionSpec as P

ITERS = 4


def shards(cost, plan, row_mass, col_mass, row_dual, col_dual):
    wide_count = lax.axis_size("wide")
    narrow_count = lax.axis_size("narrow")
    total_rows = plan.shape[0] * wide_count
    total_cols = plan.shape[1] * narrow_count
    step_base = 0.9 / math.sqrt(total_rows + total_cols)
    weight = jnp.float32(step_base)
    for step in range(ITERS):
        primal_step = step_base / weight
        dual_step = step_base * weight
        fresh = jnp.maximum(
            plan - primal_step * (cost - row_dual[:, None] - col_dual[None, :]), 0.0
        )
        change = fresh - plan
        extrap = fresh + change
        moved = jnp.sum(change * change)
        row_total = lax.psum(jnp.sum(extrap, axis=1), "narrow")
        new_row = row_dual + dual_step * (row_mass - row_total)
        row_square = jnp.sum((new_row - row_dual) ** 2)
        col_local = jnp.sum(extrap, axis=0)
        col_total = lax.psum(col_local, "wide")
        new_col = col_dual + dual_step * (col_mass - col_total)
        col_share = jnp.sum((new_col - col_dual) ** 2) / wide_count
        dual_share = row_square / narrow_count + col_share
        moved_all = lax.psum(moved, ("wide", "narrow"))
        dual_moved = lax.psum(dual_share, ("wide", "narrow"))
        weight = jnp.sqrt(weight * jnp.sqrt((dual_moved + 1.0) / (moved_all + 1.0)))
        plan, row_dual, col_dual = (fresh, new_row, new_col)
    return (plan, row_dual, col_dual)


def solution(mesh):
    in_specs = (
        P("wide", "narrow"),
        P("wide", "narrow"),
        P("wide"),
        P("narrow"),
        P("wide"),
        P("narrow"),
    )
    out_specs = (P("wide", "narrow"), P("wide"), P("narrow"))
    return jax.shard_map(shards, mesh=mesh, in_specs=in_specs, out_specs=out_specs, check_vma=False)
```

profile of v0, /device:TPU:0, one launch (start us, length us, event | category | flops | bytes accessed | tf_op | source)
XLA Modules:
  0.0 314.4 jit_solution(7714371782723744070)
XLA Ops:
  0.6 0.0 copy-start.1
  0.6 0.0 copy-start.3
  0.7 0.0 copy-start.2
  0.7 0.0 copy-start.4
  0.7 0.0 copy-start
  0.7 4.2 %multiply_reduce_fusion.2 = (f32[]{:T(128)}, f32[4096]{0:T(1024)S(1)}, f32[128]{0:T(128)S(1)}) fusion(f32[128,4096]{1,0:T(8,128)} %param.7, f32[4096]{0:T(1024)} %param.11, f32[128,4096]{1,0:T(8,128)} %param.6, f32[128]{0:T(128)} %param.10), kind=kLoop, calls=%fused_computation.6 | loop fusion | flops 5238655 | bytes 4228100 | tf_op jit(solution)/shard_map/reduce_sum | solution.py:25
  4.9 38.8 %psum.99 = f32[4096]{0:T(1024)S(1)} all-reduce(f32[4096]{0:T(1024)S(1)} %get-tuple-element.12), channel_id=1, replica_groups=mesh['wide'=8,'narrow'=4] {'wide'}, use_global_device_ids=true, to_apply=%region_4.0 | all-reduce | flops 4096 | bytes 32768 | tf_op jit(solution)/shard_map/psum | solution.py:30
  43.7 5.6 %psum.98 = f32[128]{0:T(128)S(1)} all-reduce(f32[128]{0:T(128)S(1)} %get-tuple-element.13), channel_id=1, replica_groups=mesh['wide'=8,'narrow'=4] {'narrow'}, use_global_device_ids=true, to_apply=%region_1.0 | all-reduce | flops 128 | bytes 1024 | tf_op jit(solution)/shard_map/psum | solution.py:26
  49.3 0.0 copy-done.3
  49.3 0.0 copy-done.4
  49.3 0.6 multiply_reduce_fusion.8
  50.6 0.0 copy-done.1
  50.6 0.0 copy-done.2
  50.6 0.6 multiply_reduce_fusion.5
  51.9 37.2 %all-reduce.2 = (f32[]{:T(128)}, f32[]{:T(128)}) all-reduce(f32[]{:T(128)S(6)} %add.94, f32[]{:T(128)} %get-tuple-element.11), channel_id=1, replica_groups=mesh['wide'=8,'narrow'=4] {'wide','narrow'}, use_global_device_ids=true, to_apply=%region_6.0 | all-reduce | flops 2 | bytes 16 | tf_op jit(solution)/shard_map/psum | solution.py:35
  90.5 0.0 copy-done
  90.5 3.7 %multiply_reduce_fusion.1 = (f32[]{:T(128)}, f32[128]{0:T(128)S(1)}, f32[4096]{0:T(1024)S(1)}) fusion(f32[4096]{0:T(1024)S(1)} %get-tuple-element.30, f32[128,4096]{1,0:T(8,128)} %param.6, f32[128]{0:T(128)S(1)} %get-tuple-element.32, f32[]{:T(128)S(6)} %div.39, f32[128,4096]{1,0:T(8,128)S(1)} %copy-done, f32[4096]{0:T(1024)S(1)} %copy-done.1, ...), kind=kLoop, calls=%fused_computation.4 | loop fusion | flops 7860095 | bytes 4245000 | tf_op jit(solution)/shard_map/reduce_sum | solution.py:25
  94.2 6.9 %psum.102 = f32[128]{0:T(128)S(1)} all-reduce(f32[128]{0:T(128)S(1)} %get-tuple-element.9), channel_id=1, replica_groups=mesh['wide'=8,'narrow'=4] {'narrow'}, use_global_device_ids=true, to_apply=%region_10.0 | all-reduce | flops 128 | bytes 1024 | tf_op jit(solution)/shard_map/psum | solution.py:26
  101.1 0.6 multiply_reduce_fusion.7
  102.4 35.6 %psum.103 = f32[4096]{0:T(1024)S(1)} all-reduce(f32[4096]{0:T(1024)S(1)} %get-tuple-element.10), channel_id=1, replica_groups=mesh['wide'=8,'narrow'=4] {'wide'}, use_global_device_ids=true, to_apply=%region_13.0 | all-reduce | flops 4096 | bytes 32768 | tf_op jit(solution)/shard_map/psum | solution.py:30
  138.0 0.6 multiply_reduce_fusion.4
  139.2 37.1 %all-reduce.1 = (f32[]{:T(128)}, f32[]{:T(128)}) all-reduce(f32[]{:T(128)S(6)} %add.100, f32[]{:T(128)} %get-tuple-element.8), channel_id=1, replica_groups=mesh['wide'=8,'narrow'=4] {'wide','narrow'}, use_global_device_ids=true, to_apply=%region_15.0 | all-reduce | flops 2 | bytes 16 | tf_op jit(solution)/shard_map/psum | solution.py:35
  177.8 4.2 %multiply_reduce_fusion = (f32[]{:T(128)}, f32[128]{0:T(128)S(1)}, f32[4096]{0:T(1024)S(1)}) fusion(f32[4096]{0:T(1024)S(1)} %get-tuple-element.26, f32[128,4096]{1,0:T(8,128)} %param.6, f32[128]{0:T(128)S(1)} %get-tuple-element.28, f32[]{:T(128)S(6)} %div.43, f32[4096]{0:T(1024)S(1)} %get-tuple-element.30, f32[128]{0:T(128)S(1)} %get-tuple-element.32, ...), kind=kLoop, calls=%fused_computation.2 | loop fusion | flops 10481535 | bytes 4261900 | tf_op jit(solution)/shard_map/reduce_sum | solution.py:25
  182.0 7.2 %psum.106 = f32[128]{0:T(128)S(1)} all-reduce(f32[128]{0:T(128)S(1)} %get-tuple-element.6), channel_id=1, replica_groups=mesh['wide'=8,'narrow'=4] {'narrow'}, use_global_device_ids=true, to_apply=%region_19.0 | all-reduce | flops 128 | bytes 1024 | tf_op jit(solution)/shard_map/psum | solution.py:26
  189.2 0.6 multiply_reduce_fusion.6
  190.5 35.3 %psum.107 = f32[4096]{0:T(1024)S(1)} all-reduce(f32[4096]{0:T(1024)S(1)} %get-tuple-element.7), channel_id=1, replica_groups=mesh['wide'=8,'narrow'=4] {'wide'}, use_global_device_ids=true, to_apply=%region_22.0 | all-reduce | flops 4096 | bytes 32768 | tf_op jit(solution)/shard_map/psum | solution.py:30
  225.8 0.6 multiply_reduce_fusion.3
  227.0 37.3 %all-reduce = (f32[]{:T(128)}, f32[]{:T(128)}) all-reduce(f32[]{:T(128)S(6)} %add.106, f32[]{:T(128)} %get-tuple-element.5), channel_id=1, replica_groups=mesh['wide'=8,'narrow'=4] {'wide','narrow'}, use_global_device_ids=true, to_apply=%region_24.0 | all-reduce | flops 2 | bytes 16 | tf_op jit(solution)/shard_map/psum | solution.py:35
  265.8 4.9 %fusion.6 = (f32[4096]{0:T(1024)S(1)}, f32[128]{0:T(128)S(1)}, f32[128,4096]{1,0:T(8,128)}) fusion(f32[4096]{0:T(1024)S(1)} %get-tuple-element.26, f32[128,4096]{1,0:T(8,128)} %param.6, f32[128]{0:T(128)S(1)} %get-tuple-element.28, f32[]{:T(128)S(6)} %div.43, f32[4096]{0:T(1024)S(1)} %get-tuple-element.30, f32[128]{0:T(128)S(1)} %get-tuple-element.32, ...), kind=kLoop, calls=%fused_computation.17 | loop fusion | flops 12054400 | bytes 6375948 | tf_op jit(solution)/shard_map/reduce_sum | solution.py:29
  270.7 36.8 %psum.111 = f32[4096]{0:T(1024)S(1)} all-reduce(f32[4096]{0:T(1024)S(1)} %get-tuple-element.3), channel_id=1, replica_groups=mesh['wide'=8,'narrow'=4] {'wide'}, use_global_device_ids=true, to_apply=%region_30.0 | all-reduce | flops 4096 | bytes 32768 | tf_op jit(solution)/shard_map/psum | solution.py:30
  307.5 0.6 multiply_add_fusion
  308.1 5.7 %psum.110 = f32[128]{0:T(128)S(1)} all-reduce(f32[128]{0:T(128)S(1)} %get-tuple-element.4), channel_id=1, replica_groups=mesh['wide'=8,'narrow'=4] {'narrow'}, use_global_device_ids=true, to_apply=%region_28.0 | all-reduce | flops 128 | bytes 1024 | tf_op jit(solution)/shard_map/psum | solution.py:26
  313.9 0.5 multiply_add_fusion.4
Async XLA Ops:
  0.6 49.9 %copy-start.1 = (f32[4096]{0:T(1024)S(1)}, f32[4096]{0:T(1024)}, u32[]{:S(2)}) copy-start(f32[4096]{0:T(1024)} %param.11) | copy-start | bytes 49156
  0.6 48.7 %copy-start.3 = (f32[128]{0:T(128)S(1)}, f32[128]{0:T(128)}, u32[]{:S(2)}) copy-start(f32[128]{0:T(128)} %param.10) | copy-start | bytes 1540
  0.7 49.9 %copy-start.2 = (f32[4096]{0:T(1024)S(1)}, f32[4096]{0:T(1024)}, u32[]{:S(2)}) copy-start(f32[4096]{0:T(1024)} %param.9) | copy-start | bytes 49156
  0.7 48.7 %copy-start.4 = (f32[128]{0:T(128)S(1)}, f32[128]{0:T(128)}, u32[]{:S(2)}) copy-start(f32[128]{0:T(128)} %param.8) | copy-start | bytes 1540
  0.7 89.8 %copy-start = (f32[128,4096]{1,0:T(8,128)S(1)}, f32[128,4096]{1,0:T(8,128)}, u32[]{:S(2)}) copy-start(f32[128,4096]{1,0:T(8,128)} %param.7) | copy-start | bytes 6291460
where the time goes:
time: 315 us; the launch traced here: 314 us
  blocking collectives  284 us (90%)
  other arithmetic  21.7 us (7%)
  between operations  9.03 us (3%)
    psum x4, blocking collectives, shards(): col_total = lax.psum(col_local, 'wide')  147 us
    psum x3, blocking collectives, shards(): dual_moved = lax.psum(dual_share, ('wide', 'narrow'))  112 us
    psum x4, blocking collectives, shards(): row_total = lax.psum(jnp.sum(extrap, axis=1), 'narrow')  25.5 us
    reduce_sum x3, other arithmetic, shards(): moved = jnp.sum(change * change)  12.1 us

commit v1 on v0

--- a/solution.py
+++ b/solution.py
@@ -27,7 +27,11 @@
         new_row = row_dual + dual_step * (row_mass - row_total)
         row_square = jnp.sum((new_row - row_dual) ** 2)
         col_local = jnp.sum(extrap, axis=0)
-        col_total = lax.psum(col_local, "wide")
+        col_total = col_local
+        for hop in (1, 2, 4):
+            col_total = col_total + lax.ppermute(
+                col_total, "wide", [(dev, dev ^ hop) for dev in range(8)]
+            )
         new_col = col_dual + dual_step * (col_mass - col_total)
         col_share = jnp.sum((new_col - col_dual) ** 2) / wide_count
         dual_share = row_square / narrow_count + col_share

time: 315 us -> 211 us (0.67)
  blocking collectives: 284 us -> 145 us
  starting transfers between devices: 0 us -> 23.2 us
  waiting for transfers between devices: 0 us -> 11.4 us
    psum x4 -> x0, blocking collectives: 147 us -> none  [shards(): col_total = lax.psum(col_local, 'wide')]
    ppermute x0 -> x12, starting transfers between devices: none -> 23.2 us  [shards(): lax.ppermute(col_total, 'wide', [(dev, dev ^ hop) for dev in range(8)])]
    ppermute x0 -> x12, waiting for transfers between devices: none -> 11.4 us  [shards(): lax.ppermute(col_total, 'wide', [(dev, dev ^ hop) for dev in range(8)])]
    psum x3, blocking collectives: 112 us -> 122 us  [shards(): dual_moved = lax.psum(dual_share, ('wide', 'narrow'))]
  transfers between devices with their start and end apart: 0 -> 12, of which waited for: 0 -> 8; matrix products, arithmetic and copies ran while one was open for 0% -> 1% of each run, Pallas kernels for 0% -> 0%
where the time goes in v1:
time: 211 us
  blocking collectives  145 us (69%)
  starting transfers between devices  23.2 us (11%)
  other arithmetic  21.8 us (10%)
  waiting for transfers between devices  11.4 us (5%)
  between operations  9.03 us (4%)
    psum x3, blocking collectives, shards(): dual_moved = lax.psum(dual_share, ('wide', 'narrow'))  122 us
    ppermute x12, starting transfers between devices, shards(): lax.ppermute(col_total, 'wide', [(dev, dev ^ hop) for dev in range(8)])  23.2 us
    psum x4, blocking collectives, shards(): row_total = lax.psum(jnp.sum(extrap, axis=1), 'narrow')  22.8 us
    reduce_sum x3, other arithmetic, shards(): moved = jnp.sum(change * change)  12.1 us
    ppermute x12, waiting for transfers between devices, shards(): lax.ppermute(col_total, 'wide', [(dev, dev ^ hop) for dev in range(8)])  11.4 us
    reduce_sum x1, other arithmetic, shards(): col_local = jnp.sum(extrap, axis=0)  4.91 us
  transfers between devices with their start and end apart: 12, of which 8 were waited for; matrix products, arithmetic and copies ran while one was open for 1% of the time, Pallas kernels for 0%

profile of v1, /device:TPU:0, one launch (start us, length us, event | category | flops | bytes accessed | tf_op | source)
XLA Modules:
  0.0 210.6 jit_solution(1587586112322570426)
XLA Ops:
  0.6 0.0 copy-start.1
  0.6 0.0 copy-start.3
  0.7 0.0 copy-start
  0.7 4.2 %multiply_reduce_fusion.2 = (f32[]{:T(128)}, f32[4096]{0:T(1024)S(1)}, f32[128]{0:T(128)S(1)}) fusion(f32[128,4096]{1,0:T(8,128)} %param.7, f32[4096]{0:T(1024)} %param.11, f32[128,4096]{1,0:T(8,128)} %param.6, f32[128]{0:T(128)} %param.10), kind=kLoop, calls=%fused_computation.6 | loop fusion | flops 5238655 | bytes 4228100 | tf_op jit(solution)/shard_map/reduce_sum | solution.py:25
  4.8 3.0 %collective-permute-start = (f32[4096]{0:T(1024)S(1)}, f32[4096]{0:T(1024)S(1)}, u32[]{:S(2)}, u32[]{:S(2)}) collective-permute-start(f32[4096]{0:T(1024)S(1)} %get-tuple-element.12), channel_id=1, source_target_pairs={{0,4},{4,0},{8,12},{12,8},{16,20},{20,16},{24,28},{28,24},{1,5},{5... | collective-permute-start | bytes 49160 | tf_op jit(solution)/shard_map/ppermute | solution.py:32
  7.8 1.7 collective-permute-done
  9.5 2.1 %collective-permute-start.1 = (f32[4096]{0:T(1024)S(1)}, f32[4096]{0:T(1024)S(1)}, u32[]{:S(2)}, u32[]{:S(2)}) collective-permute-start(f32[4096]{0:T(1024)S(1)} %add.121), channel_id=1, source_target_pairs={{0,8},{4,12},{8,0},{12,4},{16,24},{20,28},{24,16},{28,20},{1,9},{5... | collective-permute-start | bytes 49160 | tf_op jit(solution)/shard_map/ppermute | solution.py:32
  11.6 5.6 %psum.70 = f32[128]{0:T(128)S(1)} all-reduce(f32[128]{0:T(128)S(1)} %get-tuple-element.13), channel_id=1, replica_groups=mesh['wide'=8,'narrow'=4] {'narrow'}, use_global_device_ids=true, to_apply=%region_1.0 | all-reduce | flops 128 | bytes 1024 | tf_op jit(solution)/shard_map/psum | solution.py:26
  17.3 0.0 collective-permute-done.1
  17.3 2.7 %collective-permute-start.2 = (f32[4096]{0:T(1024)S(1)}, f32[4096]{0:T(1024)S(1)}, u32[]{:S(2)}, u32[]{:S(2)}) collective-permute-start(f32[4096]{0:T(1024)S(1)} %add.122), channel_id=1, source_target_pairs={{0,16},{4,20},{8,24},{12,28},{16,0},{20,4},{24,8},{28,12},{1,17},{... | collective-permute-start | bytes 49160 | tf_op jit(solution)/shard_map/ppermute | solution.py:32
  19.9 0.0 copy-done.3
  19.9 0.6 multiply_reduce_fusion.8
  21.2 0.8 collective-permute-done.2
  22.0 0.0 copy-done.2
  22.0 0.6 multiply_reduce_fusion.5
  23.3 40.9 %all-reduce.2 = (f32[]{:T(128)}, f32[]{:T(128)}) all-reduce(f32[]{:T(128)S(6)} %add.125, f32[]{:T(128)} %get-tuple-element.11), channel_id=1, replica_groups=mesh['wide'=8,'narrow'=4] {'wide','narrow'}, use_global_device_ids=true, to_apply=%region_5.0 | all-reduce | flops 2 | bytes 16 | tf_op jit(solution)/shard_map/psum | solution.py:39
  65.6 3.7 %multiply_reduce_fusion.1 = (f32[]{:T(128)}, f32[128]{0:T(128)S(1)}, f32[4096]{0:T(1024)S(1)}) fusion(f32[4096]{0:T(1024)S(1)} %get-tuple-element.30, f32[128,4096]{1,0:T(8,128)} %param.6, f32[128]{0:T(128)S(1)} %get-tuple-element.32, f32[]{:T(128)S(6)} %div.39, f32[128,4096]{1,0:T(8,128)S(1)} %copy-done, f32[4096]{0:T(1024)S(1)} %copy-done.1, ...), kind=kLoop, calls=%fused_computation.4 | loop fusion | flops 7860095 | bytes 4245000 | tf_op jit(solution)/shard_map/reduce_sum | solution.py:25
  69.3 2.3 %collective-permute-start.3 = (f32[4096]{0:T(1024)S(1)}, f32[4096]{0:T(1024)S(1)}, u32[]{:S(2)}, u32[]{:S(2)}) collective-permute-start(f32[4096]{0:T(1024)S(1)} %get-tuple-element.10), channel_id=1, source_target_pairs={{0,4},{4,0},{8,12},{12,8},{16,20},{20,16},{24,28},{28,24},{1,5},{5... | collective-permute-start | bytes 49160 | tf_op jit(solution)/shard_map/ppermute | solution.py:32
  71.6 1.7 collective-permute-done.3
  73.3 0.5 collective-permute-start.4
  73.8 5.7 %psum.73 = f32[128]{0:T(128)S(1)} all-reduce(f32[128]{0:T(128)S(1)} %get-tuple-element.9), channel_id=1, replica_groups=mesh['wide'=8,'narrow'=4] {'narrow'}, use_global_device_ids=true, to_apply=%region_9.0 | all-reduce | flops 128 | bytes 1024 | tf_op jit(solution)/shard_map/psum | solution.py:26
  79.5 0.0 collective-permute-done.4
  79.5 2.5 %collective-permute-start.5 = (f32[4096]{0:T(1024)S(1)}, f32[4096]{0:T(1024)S(1)}, u32[]{:S(2)}, u32[]{:S(2)}) collective-permute-start(f32[4096]{0:T(1024)S(1)} %add.131), channel_id=1, source_target_pairs={{0,16},{4,20},{8,24},{12,28},{16,0},{20,4},{24,8},{28,12},{1,17},{... | collective-permute-start | bytes 49160 | tf_op jit(solution)/shard_map/ppermute | solution.py:32
  82.0 0.6 multiply_reduce_fusion.7
  83.2 1.0 collective-permute-done.5
  84.2 0.6 multiply_reduce_fusion.4
  85.5 40.3 %all-reduce.1 = (f32[]{:T(128)}, f32[]{:T(128)}) all-reduce(f32[]{:T(128)S(6)} %add.134, f32[]{:T(128)} %get-tuple-element.8), channel_id=1, replica_groups=mesh['wide'=8,'narrow'=4] {'wide','narrow'}, use_global_device_ids=true, to_apply=%region_13.0 | all-reduce | flops 2 | bytes 16 | tf_op jit(solution)/shard_map/psum | solution.py:39
  127.3 4.2 %multiply_reduce_fusion = (f32[]{:T(128)}, f32[128]{0:T(128)S(1)}, f32[4096]{0:T(1024)S(1)}) fusion(f32[4096]{0:T(1024)S(1)} %get-tuple-element.26, f32[128,4096]{1,0:T(8,128)} %param.6, f32[128]{0:T(128)S(1)} %get-tuple-element.28, f32[]{:T(128)S(6)} %div.43, f32[4096]{0:T(1024)S(1)} %get-tuple-element.30, f32[128]{0:T(128)S(1)} %get-tuple-element.32, ...), kind=kLoop, calls=%fused_computation.2 | loop fusion | flops 10481535 | bytes 4261900 | tf_op jit(solution)/shard_map/reduce_sum | solution.py:25
  131.4 2.3 %collective-permute-start.6 = (f32[4096]{0:T(1024)S(1)}, f32[4096]{0:T(1024)S(1)}, u32[]{:S(2)}, u32[]{:S(2)}) collective-permute-start(f32[4096]{0:T(1024)S(1)} %get-tuple-element.7), channel_id=1, source_target_pairs={{0,4},{4,0},{8,12},{12,8},{16,20},{20,16},{24,28},{28,24},{1,5},{5... | collective-permute-start | bytes 49160 | tf_op jit(solution)/shard_map/ppermute | solution.py:32
  133.7 1.7 collective-permute-done.6
  135.4 0.4 collective-permute-start.7
  135.9 5.7 %psum.76 = f32[128]{0:T(128)S(1)} all-reduce(f32[128]{0:T(128)S(1)} %get-tuple-element.6), channel_id=1, replica_groups=mesh['wide'=8,'narrow'=4] {'narrow'}, use_global_device_ids=true, to_apply=%region_17.0 | all-reduce | flops 128 | bytes 1024 | tf_op jit(solution)/shard_map/psum | solution.py:26
  141.6 0.0 collective-permute-done.7
  141.6 2.4 %collective-permute-start.8 = (f32[4096]{0:T(1024)S(1)}, f32[4096]{0:T(1024)S(1)}, u32[]{:S(2)}, u32[]{:S(2)}) collective-permute-start(f32[4096]{0:T(1024)S(1)} %add.140), channel_id=1, source_target_pairs={{0,16},{4,20},{8,24},{12,28},{16,0},{20,4},{24,8},{28,12},{1,17},{... | collective-permute-start | bytes 49160 | tf_op jit(solution)/shard_map/ppermute | solution.py:32
  144.0 0.6 multiply_reduce_fusion.6
  145.3 1.1 collective-permute-done.8
  146.3 0.6 multiply_reduce_fusion.3
  147.6 41.2 %all-reduce = (f32[]{:T(128)}, f32[]{:T(128)}) all-reduce(f32[]{:T(128)S(6)} %add.143, f32[]{:T(128)} %get-tuple-element.5), channel_id=1, replica_groups=mesh['wide'=8,'narrow'=4] {'wide','narrow'}, use_global_device_ids=true, to_apply=%region_21.0 | all-reduce | flops 2 | bytes 16 | tf_op jit(solution)/shard_map/psum | solution.py:39
  190.2 4.9 %fusion.6 = (f32[4096]{0:T(1024)S(1)}, f32[128]{0:T(128)S(1)}, f32[128,4096]{1,0:T(8,128)}) fusion(f32[4096]{0:T(1024)S(1)} %get-tuple-element.26, f32[128,4096]{1,0:T(8,128)} %param.6, f32[128]{0:T(128)S(1)} %get-tuple-element.28, f32[]{:T(128)S(6)} %div.43, f32[4096]{0:T(1024)S(1)} %get-tuple-element.30, f32[128]{0:T(128)S(1)} %get-tuple-element.32, ...), kind=kLoop, calls=%fused_computation.17 | loop fusion | flops 12054400 | bytes 6375948 | tf_op jit(solution)/shard_map/reduce_sum | solution.py:29
  195.1 2.3 %collective-permute-start.9 = (f32[4096]{0:T(1024)S(1)}, f32[4096]{0:T(1024)S(1)}, u32[]{:S(2)}, u32[]{:S(2)}) collective-permute-start(f32[4096]{0:T(1024)S(1)} %get-tuple-element.3), channel_id=1, source_target_pairs={{0,4},{4,0},{8,12},{12,8},{16,20},{20,16},{24,28},{28,24},{1,5},{5... | collective-permute-start | bytes 49160 | tf_op jit(solution)/shard_map/ppermute | solution.py:32
  197.4 1.7 collective-permute-done.9
  199.1 0.4 collective-permute-start.10
  199.5 5.7 %psum.79 = f32[128]{0:T(128)S(1)} all-reduce(f32[128]{0:T(128)S(1)} %get-tuple-element.4), channel_id=1, replica_groups=mesh['wide'=8,'narrow'=4] {'narrow'}, use_global_device_ids=true, to_apply=%region_25.0 | all-reduce | flops 128 | bytes 1024 | tf_op jit(solution)/shard_map/psum | solution.py:26
  205.3 0.0 collective-permute-done.10
  205.3 2.5 %collective-permute-start.11 = (f32[4096]{0:T(1024)S(1)}, f32[4096]{0:T(1024)S(1)}, u32[]{:S(2)}, u32[]{:S(2)}) collective-permute-start(f32[4096]{0:T(1024)S(1)} %add.149), channel_id=1, source_target_pairs={{0,16},{4,20},{8,24},{12,28},{16,0},{20,4},{24,8},{28,12},{1,17},{... | collective-permute-start | bytes 49160 | tf_op jit(solution)/shard_map/ppermute | solution.py:32
  207.8 0.5 multiply_add_fusion.4
  208.3 1.7 collective-permute-done.11
  210.0 0.6 multiply_add_fusion
  (13 shorter events, 0.0 us)
Async XLA Ops:
  0.6 21.4 %copy-start.1 = (f32[4096]{0:T(1024)S(1)}, f32[4096]{0:T(1024)}, u32[]{:S(2)}) copy-start(f32[4096]{0:T(1024)} %param.11) | copy-start | bytes 49156
  0.6 19.3 %copy-start.3 = (f32[128]{0:T(128)S(1)}, f32[128]{0:T(128)}, u32[]{:S(2)}) copy-start(f32[128]{0:T(128)} %param.10) | copy-start | bytes 1540
  0.7 65.0 %copy-start = (f32[128,4096]{1,0:T(8,128)S(1)}, f32[128,4096]{1,0:T(8,128)}, u32[]{:S(2)}) copy-start(f32[128,4096]{1,0:T(8,128)} %param.7) | copy-start | bytes 6291460
  0.7 19.3 %copy-start.4 = (f32[128]{0:T(128)S(1)}, f32[128]{0:T(128)}, u32[]{:S(2)}) copy-start(f32[128]{0:T(128)} %param.8) | copy-start | bytes 1540
  0.7 21.3 %copy-start.2 = (f32[4096]{0:T(1024)S(1)}, f32[4096]{0:T(1024)}, u32[]{:S(2)}) copy-start(f32[4096]{0:T(1024)} %param.9) | copy-start | bytes 49156
  4.8 4.7 %collective-permute-start = (f32[4096]{0:T(1024)S(1)}, f32[4096]{0:T(1024)S(1)}, u32[]{:S(2)}, u32[]{:S(2)}) collective-permute-start(f32[4096]{0:T(1024)S(1)} %get-tuple-element.12), channel_id=1, source_target_pairs={{0,4},{4,0},{8,12},{12,8},{16,20},{20,16},{24,28},{28,24},{1,5},{5... | collective-permute-start | bytes 49160 | tf_op jit(solution)/shard_map/ppermute | solution.py:32
  9.5 7.7 %collective-permute-start.1 = (f32[4096]{0:T(1024)S(1)}, f32[4096]{0:T(1024)S(1)}, u32[]{:S(2)}, u32[]{:S(2)}) collective-permute-start(f32[4096]{0:T(1024)S(1)} %add.121), channel_id=1, source_target_pairs={{0,8},{4,12},{8,0},{12,4},{16,24},{20,28},{24,16},{28,20},{1,9},{5... | collective-permute-start | bytes 49160 | tf_op jit(solution)/shard_map/ppermute | solution.py:32
  17.3 4.7 %collective-permute-start.2 = (f32[4096]{0:T(1024)S(1)}, f32[4096]{0:T(1024)S(1)}, u32[]{:S(2)}, u32[]{:S(2)}) collective-permute-start(f32[4096]{0:T(1024)S(1)} %add.122), channel_id=1, source_target_pairs={{0,16},{4,20},{8,24},{12,28},{16,0},{20,4},{24,8},{28,12},{1,17},{... | collective-permute-start | bytes 49160 | tf_op jit(solution)/shard_map/ppermute | solution.py:32
  69.3 4.0 %collective-permute-start.3 = (f32[4096]{0:T(1024)S(1)}, f32[4096]{0:T(1024)S(1)}, u32[]{:S(2)}, u32[]{:S(2)}) collective-permute-start(f32[4096]{0:T(1024)S(1)} %get-tuple-element.10), channel_id=1, source_target_pairs={{0,4},{4,0},{8,12},{12,8},{16,20},{20,16},{24,28},{28,24},{1,5},{5... | collective-permute-start | bytes 49160 | tf_op jit(solution)/shard_map/ppermute | solution.py:32
  73.3 6.2 %collective-permute-start.4 = (f32[4096]{0:T(1024)S(1)}, f32[4096]{0:T(1024)S(1)}, u32[]{:S(2)}, u32[]{:S(2)}) collective-permute-start(f32[4096]{0:T(1024)S(1)} %add.130), channel_id=1, source_target_pairs={{0,8},{4,12},{8,0},{12,4},{16,24},{20,28},{24,16},{28,20},{1,9},{5... | collective-permute-start | bytes 49160 | tf_op jit(solution)/shard_map/ppermute | solution.py:32
  79.5 4.7 %collective-permute-start.5 = (f32[4096]{0:T(1024)S(1)}, f32[4096]{0:T(1024)S(1)}, u32[]{:S(2)}, u32[]{:S(2)}) collective-permute-start(f32[4096]{0:T(1024)S(1)} %add.131), channel_id=1, source_target_pairs={{0,16},{4,20},{8,24},{12,28},{16,0},{20,4},{24,8},{28,12},{1,17},{... | collective-permute-start | bytes 49160 | tf_op jit(solution)/shard_map/ppermute | solution.py:32
  131.4 4.0 %collective-permute-start.6 = (f32[4096]{0:T(1024)S(1)}, f32[4096]{0:T(1024)S(1)}, u32[]{:S(2)}, u32[]{:S(2)}) collective-permute-start(f32[4096]{0:T(1024)S(1)} %get-tuple-element.7), channel_id=1, source_target_pairs={{0,4},{4,0},{8,12},{12,8},{16,20},{20,16},{24,28},{28,24},{1,5},{5... | collective-permute-start | bytes 49160 | tf_op jit(solution)/shard_map/ppermute | solution.py:32
  135.4 6.2 %collective-permute-start.7 = (f32[4096]{0:T(1024)S(1)}, f32[4096]{0:T(1024)S(1)}, u32[]{:S(2)}, u32[]{:S(2)}) collective-permute-start(f32[4096]{0:T(1024)S(1)} %add.139), channel_id=1, source_target_pairs={{0,8},{4,12},{8,0},{12,4},{16,24},{20,28},{24,16},{28,20},{1,9},{5... | collective-permute-start | bytes 49160 | tf_op jit(solution)/shard_map/ppermute | solution.py:32
  141.6 4.7 %collective-permute-start.8 = (f32[4096]{0:T(1024)S(1)}, f32[4096]{0:T(1024)S(1)}, u32[]{:S(2)}, u32[]{:S(2)}) collective-permute-start(f32[4096]{0:T(1024)S(1)} %add.140), channel_id=1, source_target_pairs={{0,16},{4,20},{8,24},{12,28},{16,0},{20,4},{24,8},{28,12},{1,17},{... | collective-permute-start | bytes 49160 | tf_op jit(solution)/shard_map/ppermute | solution.py:32
  195.1 4.0 %collective-permute-start.9 = (f32[4096]{0:T(1024)S(1)}, f32[4096]{0:T(1024)S(1)}, u32[]{:S(2)}, u32[]{:S(2)}) collective-permute-start(f32[4096]{0:T(1024)S(1)} %get-tuple-element.3), channel_id=1, source_target_pairs={{0,4},{4,0},{8,12},{12,8},{16,20},{20,16},{24,28},{28,24},{1,5},{5... | collective-permute-start | bytes 49160 | tf_op jit(solution)/shard_map/ppermute | solution.py:32
  199.1 6.2 %collective-permute-start.10 = (f32[4096]{0:T(1024)S(1)}, f32[4096]{0:T(1024)S(1)}, u32[]{:S(2)}, u32[]{:S(2)}) collective-permute-start(f32[4096]{0:T(1024)S(1)} %add.148), channel_id=1, source_target_pairs={{0,8},{4,12},{8,0},{12,4},{16,24},{20,28},{24,16},{28,20},{1,9},{5... | collective-permute-start | bytes 49160 | tf_op jit(solution)/shard_map/ppermute | solution.py:32
  205.3 4.7 %collective-permute-start.11 = (f32[4096]{0:T(1024)S(1)}, f32[4096]{0:T(1024)S(1)}, u32[]{:S(2)}, u32[]{:S(2)}) collective-permute-start(f32[4096]{0:T(1024)S(1)} %add.149), channel_id=1, source_target_pairs={{0,16},{4,20},{8,24},{12,28},{16,0},{20,4},{24,8},{28,12},{1,17},{... | collective-permute-start | bytes 49160 | tf_op jit(solution)/shard_map/ppermute | solution.py:32
